TPU v7x, 32 devices: a whole 2x2x4 slice. The times are simulated.
32 devices in a mesh: lon: 16 (over z, y, core), lat: 2 (over x).
Axes of the slice: x: 2, y: 2, z: 4, core: 2. Of those that a mesh axis runs over, the one named last changes fastest.
Arguments:
- fine_members: bfloat16 [32, 64, 256], P(None, 'lon', 'lat'), may hold values from -6 to 6
- coarse_members: bfloat16 [128, 32, 256], P(None, 'lon', 'lat'), may hold values from -6 to 6
- increments: bfloat16 [32, 64, 256], P(None, 'lon', 'lat'), may hold values from -0.59765625 to 0.59765625
- level_weights: float32 [2], replicated, may hold values from 0.5 to 2
Outputs:
- applied: float32 [32, 64, 256], P(None, 'lon', 'lat')
All inputs are finite; a program needn't handle non-finite values.
Results may differ from a plain program's by a relative error of at most 0.0055.
Values may be sent and summed in bfloat16 or wider, within the bound.
A program may use at most 64 MiB of HBM per device.

v0:
```python
import jax
import jax.numpy as jnp
from jax import lax
from jax.sharding import PartitionSpec as P


def from_behind(block, axis, distance):
    devices = range(lax.axis_size(axis))
    route = [(i - distance, i) for i in devices if i - distance in devices]
    return lax.ppermute(block, axis, route)


def from_behind_2(value, axis, by):
    devices = lax.axis_size(axis)
    return lax.ppermute(value, axis, [(i, (i + by) % devices) for i in range(devices)])


def refine(coarse):
    left_cols = coarse[:, :-1, :]
    right_cols = coarse[:, 1:, :]
    middle = 0.5 * (left_cols + right_cols)
    stacked = jnp.stack((left_cols, middle), axis=2)
    return stacked.reshape(left_cols.shape[0], 2 * left_cols.shape[1], left_cols.shape[2])


def anomalies(members):
    return (members - jnp.mean(members, axis=0, keepdims=True)).astype(jnp.bfloat16)


def profile(distance, extent):
    ratio = distance.astype(jnp.float32) / extent
    return jnp.where(jnp.abs(distance) <= extent, 1.0 - 0.75 * ratio * ratio, 0.0)


def flatten(values):
    return values.reshape(values.shape[0], -1)


def contract(own_part, other_part):
    return lax.dot_general(
        own_part, other_part, (((0,), (0,)), ((), ())), preferred_element_type=jnp.float32
    )


def surround(source, lat_reach):
    below_rim = from_behind(source[:, :, source.shape[2] - lat_reach :], "lat", 1)
    above_rim = from_behind(source[:, :, :lat_reach], "lat", -1)
    column = jnp.concatenate((below_rim, source, above_rim), axis=2)
    west_tile = from_behind_2(column, "lon", 1)
    east_tile = from_behind_2(column, "lon", -1)
    return (west_tile, column, east_tile)


def per_device(fine_members, coarse_members, increments, level_weights):
    fine_count, lon_cells, lat_cells = fine_members.shape
    coarse_count = coarse_members.shape[0]
    vector_count = increments.shape[0]
    halves = lon_cells // 2
    lat_reach = lat_cells // 8
    lon_reach = lon_cells - 1
    ext_width = lat_cells + 2 * lat_reach
    fine_anom = anomalies(fine_members.astype(jnp.float32))
    folded = coarse_members.reshape(coarse_count // 2, lon_cells, lat_cells)
    payload = jnp.concatenate((fine_anom, folded, increments), axis=0)
    neighbours = surround(payload, lat_reach)
    coarse_row = jnp.concatenate(
        [
            member_tile[fine_count : fine_count + coarse_count // 2].reshape(
                coarse_count, halves, ext_width
            )
            for member_tile in neighbours
        ],
        axis=1,
    ).astype(jnp.float32)
    refined = refine(jnp.concatenate((coarse_row, coarse_row[:, -1:, :]), axis=1))
    coarse_anom = anomalies(refined)
    paired_anom = anomalies(refined[:fine_count])
    own_coarse = coarse_anom[:, lon_cells : 2 * lon_cells, lat_reach : lat_reach + lat_cells]
    own_paired = paired_anom[:, lon_cells : 2 * lon_cells, lat_reach : lat_reach + lat_cells]
    pieces = []
    for ordinal in range(3):
        member_tile = neighbours[ordinal]
        pieces.append(
            (
                member_tile[:fine_count],
                coarse_anom[:, ordinal * lon_cells : (ordinal + 1) * lon_cells],
                paired_anom[:, ordinal * lon_cells : (ordinal + 1) * lon_cells],
                member_tile[fine_count + coarse_count // 2 :],
            )
        )
    own_fine = flatten(fine_anom)
    own_coarse = flatten(own_coarse)
    own_paired = flatten(own_paired)
    weight_fine = level_weights[0] / (fine_count - 1)
    weight_coarse = level_weights[1] / (coarse_count - 1)
    weight_paired = level_weights[1] / (fine_count - 1)
    lat_profile = profile(
        jnp.arange(ext_width, dtype=jnp.int32)[None, :]
        - lat_reach
        - jnp.arange(lat_cells, dtype=jnp.int32)[:, None],
        lat_reach,
    )
    totals = jnp.zeros((vector_count, lon_cells * lat_cells), jnp.float32)
    for ordinal in range(3):
        near_fine, near_coarse, near_paired, near_vectors = pieces[ordinal]
        offset = (ordinal - 1) * lon_cells
        lon_profile = profile(
            jnp.arange(lon_cells, dtype=jnp.int32)[None, :]
            + offset
            - jnp.arange(lon_cells, dtype=jnp.int32)[:, None],
            lon_reach,
        )
        taper = (lon_profile[:, None, :, None] * lat_profile[None, :, None, :]).reshape(
            lon_cells * lat_cells, lon_cells * ext_width
        )
        gram_tile = (
            weight_fine * contract(own_fine, flatten(near_fine))
            + weight_coarse * contract(own_coarse, flatten(near_coarse))
            - weight_paired * contract(own_paired, flatten(near_paired))
        )
        tapered = (taper * gram_tile).astype(jnp.bfloat16)
        totals = totals + lax.dot_general(
            flatten(near_vectors),
            tapered,
            (((1,), (1,)), ((), ())),
            preferred_element_type=jnp.float32,
        )
    return totals.reshape(vector_count, lon_cells, lat_cells)


def solution(mesh):
    in_specs = (P(None, "lon", "lat"), P(None, "lon", "lat"), P(None, "lon", "lat"), P())
    out_specs = P(None, "lon", "lat")
    return jax.shard_map(
        per_device, mesh=mesh, in_specs=in_specs, out_specs=out_specs, check_vma=False
    )
```

profile of v0, /device:TPU:0, one launch (start us, length us, event | category | flops | bytes accessed | tf_op | source)
XLA Modules:
  0.0 69.6 jit_solution(14417261146326489568)
XLA Ops:
  0.0 0.8 %convert_reduce_fusion = f32[4,128]{1,0:T(4,128)S(1)} fusion(bf16[32,4,128]{2,1,0:T(4,128)(2,1)} %param.4), kind=kLoop, calls=%fused_computation.52 | loop fusion | flops 32256 | bytes 34816 | tf_op jit(solution)/shard_map/reduce_sum | solution.py:27
  0.8 0.8 %fusion.26 = bf16[32,4,128]{2,1,0:T(4,128)(2,1)S(1)} fusion(bf16[32,4,128]{2,1,0:T(4,128)(2,1)} %param.4, f32[4,128]{1,0:T(4,128)S(1)} %broadcast_multiply_fusion.3), kind=kLoop, calls=%fused_computation.55 | loop fusion | flops 49152 | bytes 67584 | tf_op jit(solution)/shard_map/convert_element_type | solution.py:27
  1.6 1.0 %pad_maximum_fusion.3 = bf16[128,4,128]{2,1,0:T(4,128)(2,1)S(1)} fusion(bf16[32,4,128]{2,1,0:T(4,128)(2,1)} %param.6, bf16[64,4,128]{2,1,0:T(4,128)(2,1)} %bitcast.96, bf16[32,4,128]{2,1,0:T(4,128)(2,1)S(1)} %fusion.26), kind=kLoop, calls=%fused_computation.50 | loop fusion | flops 131072 | bytes 262144 | tf_op jit(solution)/shard_map/concatenate | solution.py:64
  2.5 0.1 fusion.51
  2.7 1.3 %collective-permute-start.1 = (bf16[128,4,16]{2,1,0:T(4,128)(2,1)S(1)}, bf16[128,4,16]{2,1,0:T(4,128)(2,1)S(1)}, u32[]{:S(2)}, u32[]{:S(2)}) collective-permute-start(bf16[128,4,16]{2,1,0:T(4,128)(2,1)S(1)} %get-tuple-element.22), channel_id=1, source_target_pairs={{1,0},{3,2},{5,4},{7,6},{9,8},{11,10},{13,12},{15,14},{17,16},{19,... | collective-permute-start | bytes 49160 | tf_op jit(solution)/shard_map/ppermute | solution.py:10
  4.0 4.9 %collective-permute-start = (bf16[128,4,16]{2,1,0:T(4,128)(2,1)S(1)}, bf16[128,4,16]{2,1,0:T(4,128)(2,1)S(1)}, u32[]{:S(2)}, u32[]{:S(2)}) collective-permute-start(bf16[128,4,16]{2,1,0:T(4,128)(2,1)S(1)} %get-tuple-element.21), channel_id=1, source_target_pairs={{0,1},{2,3},{4,5},{6,7},{8,9},{10,11},{12,13},{14,15},{16,17},{18,... | collective-permute-start | bytes 49160 | tf_op jit(solution)/shard_map/ppermute | solution.py:10
  9.2 1.8 %broadcast_multiply_fusion.2 = (f32[4,128,4,160]{1,0,3,2:T(4,128)S(1)}, f32[4,128,4,160]{1,0,3,2:T(4,128)}, f32[4,128,4,160]{1,0,3,2:T(4,128)S(1)}) fusion(f32[128,160]{0,1:T(8,128)S(1)} %subtract_select_fusion, f32[4,4]{0,1:T(4,128)S(1)} %subtract_select_fusion.3, f32[4,4]{0,1:T(4,128)S(1)} %get-tuple-element.29, f32[4,4]{0,1:T(4,128)S(1)} %get-tuple-element.28), kind=kLoop, calls=%fused_computation.40 | loop fusion | flops 983040 | bytes 4014272 | tf_op jit(solution)/shard_map/mul | solution.py:113
  11.0 0.6 fusion.52
  11.6 1.2 %copy.108 = f32[80,8,4,128]{3,1,2,0:T(8,128)} copy(f32[80,8,4,128]{3,2,1,0:T(4,128)S(1)} %bitcast.83) | data formatting | bytes 2621440
  12.7 1.7 %copy.69 = f32[512,640]{1,0:T(8,128)S(1)} copy(f32[512,640]{0,1:T(8,128)} %bitcast.84) | data formatting | bytes 2621440 | tf_op jit(solution)/shard_map/mul | solution.py:113
  16.2 2.5 %copy.109 = f32[80,8,4,128]{3,1,2,0:T(8,128)} copy(f32[80,8,4,128]{3,2,1,0:T(4,128)} %bitcast.82) | data formatting | bytes 2621440
  18.7 2.8 %copy.67 = f32[512,640]{1,0:T(8,128)} copy(f32[512,640]{0,1:T(8,128)} %bitcast.85) | data formatting | bytes 2621440 | tf_op jit(solution)/shard_map/mul | solution.py:113
  21.5 1.2 %copy.110 = f32[80,8,4,128]{3,1,2,0:T(8,128)} copy(f32[80,8,4,128]{3,2,1,0:T(4,128)S(1)} %bitcast.81) | data formatting | bytes 2621440
  22.7 1.7 %copy.65 = f32[512,640]{1,0:T(8,128)S(1)} copy(f32[512,640]{0,1:T(8,128)} %bitcast.86) | data formatting | bytes 2621440 | tf_op jit(solution)/shard_map/mul | solution.py:113
  24.5 0.4 pad_maximum_fusion.2
  24.9 4.6 %collective-permute-start.3 = (bf16[128,4,160]{2,1,0:T(4,128)(2,1)S(1)}, bf16[128,4,160]{2,1,0:T(4,128)(2,1)}, u32[]{:S(2)}, u32[]{:S(2)}) collective-permute-start(bf16[128,4,160]{2,1,0:T(4,128)(2,1)S(1)} %pad_maximum_fusion.2), channel_id=1, source_target_pairs={{0,30},{2,0},{4,2},{6,4},{8,6},{10,8},{12,10},{14,12},{16,14},{18,... | collective-permute-start | bytes 491528 | tf_op jit(solution)/shard_map/ppermute | solution.py:15
  29.9 0.8 %copy.56 = bf16[128,2,160]{0,2,1:T(8,128)(2,1)} copy(bf16[128,2,160]{2,1,0:T(2,128)(2,1)S(1)} %reshape.271) | data formatting | bytes 163840 | tf_op jit(solution)/shard_map/reshape | solution.py:68
  30.7 0.1 copy.53
  30.8 0.7 %reshape.278 = bf16[32,640]{1,0:T(8,128)(2,1)} reshape(bf16[32,4,160]{2,1,0:T(4,128)(2,1)S(1)} %get-tuple-element.15) | data formatting | bytes 81920 | tf_op jit(solution)/shard_map/reshape | solution.py:36
  31.6 1.4 %convolution_multiply_fusion.6 = f32[512,640]{1,0:T(8,128)} fusion(bf16[32,640]{1,0:T(8,128)(2,1)S(1)} %reshape.279, f32[]{:T(128)} %bitcast.1, bf16[4,8,4,128]{3,2,1,0:T(4,128)(2,1)S(1)} %bitcast.90), kind=kOutput, calls=%fused_computation.12 | convolution fusion | flops 21299200 | bytes 1384452 | tf_op jit(solution)/shard_map/dot_general | solution.py:40
  33.1 0.3 collective-permute-done.3
  33.4 0.9 %slice.107 = bf16[64,4,160]{2,1,0:T(4,128)(2,1)S(1)} slice(bf16[128,4,160]{2,1,0:T(4,128)(2,1)} %collective-permute-done.3), slice={[32:96], [0:4], [0:160]} | slice | bytes 163840 | tf_op jit(solution)/shard_map/slice | solution.py:68
  34.3 0.8 %reshape.272 = bf16[128,2,160]{2,1,0:T(2,128)(2,1)} reshape(bf16[64,4,160]{2,1,0:T(4,128)(2,1)S(1)} %slice.107) | data formatting | bytes 163840 | tf_op jit(solution)/shard_map/reshape | solution.py:68
  35.2 3.0 %collective-permute-done.2 = bf16[128,4,160]{2,1,0:T(4,128)(2,1)} collective-permute-done((bf16[128,4,160]{2,1,0:T(4,128)(2,1)S(1)}, bf16[128,4,160]{2,1,0:T(4,128)(2,1)}, u32[]{:S(2)}, u32[]{:S(2)}) %collective-permute-start.2) | collective-permute-done | bytes 163872 | tf_op jit(solution)/shard_map/ppermute | solution.py:15
  38.2 1.0 %slice.105 = bf16[64,4,160]{2,1,0:T(4,128)(2,1)S(1)} slice(bf16[128,4,160]{2,1,0:T(4,128)(2,1)} %collective-permute-done.2), slice={[32:96], [0:4], [0:160]} | slice | bytes 163840 | tf_op jit(solution)/shard_map/slice | solution.py:68
  39.4 1.0 %copy.57 = bf16[128,2,160]{0,2,1:T(8,128)(2,1)S(1)} copy(bf16[128,2,160]{2,1,0:T(2,128)(2,1)} %reshape.272) | data formatting | bytes 163840 | tf_op jit(solution)/shard_map/reshape | solution.py:68
  40.4 0.1 copy.55
  40.7 0.7 %copy.54 = bf16[128,2,1,160]{0,3,2,1:T(8,128)(2,1)} copy(bf16[128,2,1,160]{3,1,0,2:T(2,128)(2,1)S(1)} %concatenate.31) | data formatting | bytes 163840 | tf_op jit(solution)/shard_map/concatenate | solution.py:66
  41.6 0.9 %maximum_convert_fusion = f32[128,6,1,160]{0,3,2,1:T(8,128)S(1)} fusion(bf16[128,2,1,160]{0,3,2,1:T(8,128)(2,1)} %copy.54, bf16[128,2,1,160]{0,3,2,1:T(8,128)(2,1)S(1)} %copy.53, bf16[128,2,1,160]{0,3,2,1:T(8,128)(2,1)S(1)} %copy.52), kind=kLoop, calls=%fused_computation.48 | loop fusion | flops 368640 | bytes 737280 | tf_op jit(solution)/shard_map/convert_element_type | solution.py:74
  42.5 0.8 %copy-done.2 = f32[128,6,1,160]{0,3,2,1:T(8,128)} copy-done((f32[128,6,1,160]{0,3,2,1:T(8,128)}, f32[128,6,1,160]{0,3,2,1:T(8,128)S(1)}, u32[]{:S(2)}) %copy-start.2) | copy-done | bytes 491544
  43.3 1.3 %fusion.43 = (f32[6,2,160]{2,1,0:T(2,128)S(1)}, f32[128,6,2,160]{0,3,2,1:T(8,128)}) fusion(f32[128,6,1,160]{0,3,2,1:T(8,128)S(1)} %fusion.24, f32[128,6,1,160]{0,3,2,1:T(8,128)S(1)} %maximum_convert_fusion), kind=kLoop, calls=%fused_computation.81 | loop fusion | flops 489600 | bytes 1973760 | tf_op jit(solution)/shard_map/reduce_sum | solution.py:27
  44.6 1.6 %fusion.18 = bf16[128,12,160]{0,2,1:T(8,128)(2,1)S(1)} fusion(f32[128,6,2,160]{0,3,2,1:T(8,128)} %get-tuple-element.8, f32[12,160]{1,0:T(8,128)S(1)} %div.67), kind=kLoop, calls=%fused_computation.34 | loop fusion | flops 491520 | bytes 1482240 | tf_op jit(solution)/shard_map/convert_element_type | solution.py:27
  46.2 0.8 %fusion.46 = (bf16[128,4,160]{0,2,1:T(8,128)(2,1)}, bf16[128,4,160]{0,2,1:T(8,128)(2,1)}, bf16[128,4,160]{0,2,1:T(8,128)(2,1)}) fusion(bf16[128,12,160]{0,2,1:T(8,128)(2,1)S(1)} %fusion.18), kind=kLoop, calls=%fused_computation.83 | loop fusion | bytes 983040 | tf_op jit(solution)/shard_map/slice | solution.py:86
  47.0 1.3 %fusion.44 = (f32[6,2,160]{2,1,0:T(2,128)S(1)}, f32[32,6,2,160]{0,3,2,1:T(8,128)}) fusion(f32[128,6,1,160]{0,3,2,1:T(8,128)S(1)} %fusion.24, f32[128,6,1,160]{0,3,2,1:T(8,128)S(1)} %copy-done.3), kind=kLoop, calls=%fused_computation.82 | loop fusion | flops 120960 | bytes 1236480 | tf_op jit(solution)/shard_map/reduce_sum | solution.py:27
  48.3 0.9 %fusion.49 = (bf16[32,4,160]{2,1,0:T(4,128)(2,1)S(1)}, bf16[32,4,160]{2,1,0:T(4,128)(2,1)S(1)}) fusion(bf16[128,4,160]{2,1,0:T(4,128)(2,1)} %collective-permute-done.3), kind=kLoop, calls=%fused_computation.86 | loop fusion | bytes 163840 | tf_op jit(solution)/shard_map/slice | solution.py:85
  49.5 1.6 %copy.60 = f32[32,6,2,160]{3,0,2,1:T(8,128)S(1)} copy(f32[32,6,2,160]{0,3,2,1:T(8,128)} %get-tuple-element.6) | data formatting | bytes 491520 | tf_op jit(solution)/shard_map/slice | solution.py:77
  51.3 0.7 %reshape.285 = bf16[32,640]{1,0:T(8,128)(2,1)} reshape(bf16[32,4,160]{2,1,0:T(4,128)(2,1)S(1)} %copy.68) | data formatting | bytes 81920 | tf_op jit(solution)/shard_map/reshape | solution.py:36
  52.2 0.9 %fusion.47 = (bf16[32,4,160]{2,1,0:T(4,128)(2,1)S(1)}, bf16[32,4,160]{2,1,0:T(4,128)(2,1)S(1)}) fusion(bf16[128,4,160]{2,1,0:T(4,128)(2,1)} %collective-permute-done.2), kind=kLoop, calls=%fused_computation.84 | loop fusion | bytes 163840 | tf_op jit(solution)/shard_map/slice | solution.py:85
  53.2 2.3 %convolution_multiply_fusion = f32[512,640]{1,0:T(8,128)} fusion(bf16[128,512]{0,1:T(8,128)(2,1)S(1)} %bitcast.87, bf16[128,640]{0,1:T(8,128)(2,1)} %bitcast.95, f32[]{:T(128)} %bitcast.2), kind=kOutput, calls=%fused_computation | convolution fusion | flops 84213760 | bytes 1605636 | tf_op jit(solution)/shard_map/dot_general | solution.py:40
  55.6 1.4 %convolution_multiply_fusion.2 = f32[512,640]{1,0:T(8,128)} fusion(bf16[128,512]{0,1:T(8,128)(2,1)S(1)} %bitcast.88, bf16[128,640]{0,1:T(8,128)(2,1)S(1)} %bitcast.94, f32[]{:T(128)} %bitcast.2), kind=kOutput, calls=%fused_computation.4 | convolution fusion | flops 84213760 | bytes 1605636 | tf_op jit(solution)/shard_map/dot_general | solution.py:40
  57.1 0.7 %reshape.277 = bf16[32,640]{1,0:T(8,128)(2,1)} reshape(bf16[32,4,160]{2,1,0:T(4,128)(2,1)S(1)} %copy.64) | data formatting | bytes 81920 | tf_op jit(solution)/shard_map/reshape | solution.py:36
  57.8 2.8 %fusion.5 = f32[512,640]{1,0:T(8,128)} fusion(f32[512,640]{1,0:T(8,128)} %convolution_multiply_fusion, bf16[32,640]{1,0:T(8,128)(2,1)S(1)} %reshape.283, f32[]{:T(128)} %bitcast.1, bf16[4,8,4,128]{3,2,1,0:T(4,128)(2,1)S(1)} %bitcast.91), kind=kOutput, calls=%fused_computation.10 | convolution fusion | flops 21626880 | bytes 2695172 | tf_op jit(solution)/shard_map/dot_general | solution.py:40
  60.6 1.5 %convolution_multiply_fusion.5 = f32[512,640]{1,0:T(8,128)} fusion(bf16[32,640]{1,0:T(8,128)(2,1)S(1)} %reshape.281, f32[]{:T(128)} %bitcast.7, bf16[32,12,160]{2,0,1:T(8,128)(2,1)S(1)} %fusion.25), kind=kOutput, calls=%fused_computation.11 | convolution fusion | flops 21299200 | bytes 1384452 | tf_op jit(solution)/shard_map/dot_general | solution.py:40
  62.1 1.4 %fusion.8 = f32[512,640]{1,0:T(8,128)} fusion(f32[512,640]{1,0:T(8,128)S(1)} %copy-done.1, bf16[32,640]{1,0:T(8,128)(2,1)S(1)} %reshape.269, f32[]{:T(128)} %bitcast.1, bf16[4,8,4,128]{3,2,1,0:T(4,128)(2,1)S(1)} %bitcast.92), kind=kOutput, calls=%fused_computation.17 | convolution fusion | flops 21626880 | bytes 2695172 | tf_op jit(solution)/shard_map/dot_general | solution.py:40
  63.6 1.9 %fusion.12 = f32[32,512]{1,0:T(8,128)S(1)} fusion(bf16[32,640]{1,0:T(8,128)(2,1)S(1)} %reshape.282, f32[512,640]{1,0:T(8,128)S(1)} %copy.69, f32[512,640]{1,0:T(8,128)} %fusion.5, bf16[32,640]{1,0:T(8,128)(2,1)S(1)} %copy-done.9, f32[]{:T(128)} %bitcast.7, bf16[32,12,160]{2,0,1:T(8,128)(2,1)S(1)} %fusion.25), kind=kOutput, calls=%fused_computation.24 | convolution fusion | flops 43253760 | bytes 2801668 | tf_op jit(solution)/shard_map/dot_general | solution.py:122
  65.6 2.7 %fusion.14 = f32[32,512]{1,0:T(8,128)S(1)} fusion(bf16[32,640]{1,0:T(8,128)(2,1)S(1)} %copy-done.8, f32[512,640]{1,0:T(8,128)} %copy.67, f32[512,640]{1,0:T(8,128)} %convolution_multiply_fusion.5, f32[512,640]{1,0:T(8,128)} %convolution_multiply_fusion.6, bf16[128,512]{0,1:T(8,128)(2,1)S(1)} %bitcast.89, bf16[128,640]{0,1:T(8,128)(2,1)S(1)} %bitcast.93, ...), kind=kOutput, calls=%fused_computation.26 | convolution fusion | flops 106496000 | bytes 4333572 | tf_op jit(solution)/shard_map/dot_general | solution.py:122
  68.3 0.6 fusion.16
  68.9 0.7 reshape.286
  (64 shorter events, 2.2 us)
Async XLA Ops:
  2.7 21.8 %collective-permute-start.1 = (bf16[128,4,16]{2,1,0:T(4,128)(2,1)S(1)}, bf16[128,4,16]{2,1,0:T(4,128)(2,1)S(1)}, u32[]{:S(2)}, u32[]{:S(2)}) collective-permute-start(bf16[128,4,16]{2,1,0:T(4,128)(2,1)S(1)} %get-tuple-element.22), channel_id=1, source_target_pairs={{1,0},{3,2},{5,4},{7,6},{9,8},{11,10},{13,12},{15,14},{17,16},{19,... | collective-permute-start | bytes 49160 | tf_op jit(solution)/shard_map/ppermute | solution.py:10
  4.0 20.5 %collective-permute-start = (bf16[128,4,16]{2,1,0:T(4,128)(2,1)S(1)}, bf16[128,4,16]{2,1,0:T(4,128)(2,1)S(1)}, u32[]{:S(2)}, u32[]{:S(2)}) collective-permute-start(bf16[128,4,16]{2,1,0:T(4,128)(2,1)S(1)} %get-tuple-element.21), channel_id=1, source_target_pairs={{0,1},{2,3},{4,5},{6,7},{8,9},{10,11},{12,13},{14,15},{16,17},{18,... | collective-permute-start | bytes 49160 | tf_op jit(solution)/shard_map/ppermute | solution.py:10
  9.2 1.8 %copy-start.12 = (f32[2]{0:T(128)S(1)}, f32[2]{0:T(128)}, u32[]{:S(2)}) copy-start(f32[2]{0:T(128)} %param.7) | copy-start | bytes 28
  22.7 1.8 %copy-start.7 = (bf16[128,2,128]{2,1,0:T(2,128)(2,1)S(1)}, bf16[128,2,128]{2,1,0:T(2,128)(2,1)}, u32[]{:S(2)}) copy-start(bf16[128,2,128]{2,1,0:T(2,128)(2,1)} %param.5) | copy-start | bytes 196612
  22.7 1.8 %copy-start.11 = (bf16[32,4,128]{2,1,0:T(4,128)(2,1)S(1)}, bf16[32,4,128]{2,1,0:T(4,128)(2,1)}, u32[]{:S(2)}) copy-start(bf16[32,4,128]{2,1,0:T(4,128)(2,1)} %param.6) | copy-start | bytes 98308
  24.9 8.5 %collective-permute-start.3 = (bf16[128,4,160]{2,1,0:T(4,128)(2,1)S(1)}, bf16[128,4,160]{2,1,0:T(4,128)(2,1)}, u32[]{:S(2)}, u32[]{:S(2)}) collective-permute-start(bf16[128,4,160]{2,1,0:T(4,128)(2,1)S(1)} %pad_maximum_fusion.2), channel_id=1, source_target_pairs={{0,30},{2,0},{4,2},{6,4},{8,6},{10,8},{12,10},{14,12},{16,14},{18,... | collective-permute-start | bytes 491528 | tf_op jit(solution)/shard_map/ppermute | solution.py:15
  29.5 8.7 %collective-permute-start.2 = (bf16[128,4,160]{2,1,0:T(4,128)(2,1)S(1)}, bf16[128,4,160]{2,1,0:T(4,128)(2,1)}, u32[]{:S(2)}, u32[]{:S(2)}) collective-permute-start(bf16[128,4,160]{2,1,0:T(4,128)(2,1)S(1)} %pad_maximum_fusion.2), channel_id=1, source_target_pairs={{0,2},{2,4},{4,6},{6,8},{8,10},{10,12},{12,14},{14,16},{16,18},{18... | collective-permute-start | bytes 491528 | tf_op jit(solution)/shard_map/ppermute | solution.py:15
  33.1 7.5 %copy-start.6 = (bf16[128,2,160]{0,2,1:T(8,128)(2,1)S(1)}, bf16[128,2,160]{0,2,1:T(8,128)(2,1)}, u32[]{:S(2)}) copy-start(bf16[128,2,160]{0,2,1:T(8,128)(2,1)} %copy.56) | copy-start | bytes 245764
  42.5 0.8 %copy-start.2 = (f32[128,6,1,160]{0,3,2,1:T(8,128)}, f32[128,6,1,160]{0,3,2,1:T(8,128)S(1)}, u32[]{:S(2)}) copy-start(f32[128,6,1,160]{0,3,2,1:T(8,128)S(1)} %maximum_convert_fusion) | copy-start | bytes 1474564
  44.6 2.4 %copy-start.3 = (f32[128,6,1,160]{0,3,2,1:T(8,128)S(1)}, f32[128,6,1,160]{0,3,2,1:T(8,128)}, u32[]{:S(2)}) copy-start(f32[128,6,1,160]{0,3,2,1:T(8,128)} %copy-done.2) | copy-start | bytes 1474564
  51.2 4.3 %copy-start.5 = (bf16[128,4,160]{0,2,1:T(8,128)(2,1)S(1)}, bf16[128,4,160]{0,2,1:T(8,128)(2,1)}, u32[]{:S(2)}) copy-start(bf16[128,4,160]{0,2,1:T(8,128)(2,1)} %get-tuple-element.9) | copy-start | bytes 491524
  60.6 1.5 %copy-start.1 = (f32[512,640]{1,0:T(8,128)S(1)}, f32[512,640]{1,0:T(8,128)}, u32[]{:S(2)}) copy-start(f32[512,640]{1,0:T(8,128)} %convolution_multiply_fusion.2) | copy-start | bytes 3932164
  62.1 1.4 %copy-start.9 = (bf16[32,640]{1,0:T(8,128)(2,1)S(1)}, bf16[32,640]{1,0:T(8,128)(2,1)}, u32[]{:S(2)}) copy-start(bf16[32,640]{1,0:T(8,128)(2,1)} %reshape.285) | copy-start | bytes 122884
  63.5 2.0 %copy-start.4 = (bf16[128,4,160]{0,2,1:T(8,128)(2,1)S(1)}, bf16[128,4,160]{0,2,1:T(8,128)(2,1)}, u32[]{:S(2)}) copy-start(bf16[128,4,160]{0,2,1:T(8,128)(2,1)} %get-tuple-element.11) | copy-start | bytes 491524
  63.6 2.0 %copy-start.8 = (bf16[32,640]{1,0:T(8,128)(2,1)S(1)}, bf16[32,640]{1,0:T(8,128)(2,1)}, u32[]{:S(2)}) copy-start(bf16[32,640]{1,0:T(8,128)(2,1)} %reshape.278) | copy-start | bytes 122884
  65.5 2.8 %copy-start = (f32[512,640]{1,0:T(8,128)S(1)}, f32[512,640]{1,0:T(8,128)}, u32[]{:S(2)}) copy-start(f32[512,640]{1,0:T(8,128)} %fusion.8) | copy-start | bytes 3932164
  65.5 2.8 %copy-start.10 = (bf16[32,640]{1,0:T(8,128)(2,1)S(1)}, bf16[32,640]{1,0:T(8,128)(2,1)}, u32[]{:S(2)}) copy-start(bf16[32,640]{1,0:T(8,128)(2,1)} %reshape.277) | copy-start | bytes 122884
where the time goes:
time: 70.4 us; the launch traced here: 69.6 us
  local copies, waits for them, and re-layouts  26.9 us (38%)
  matrix products  16.1 us (23%)
  starting transfers between devices  10.9 us (15%)
  other arithmetic  10.2 us (14%)
  waiting for transfers between devices  3.32 us (5%)
  between operations  2.14 us (3%)
    dot_general x6, matrix products, contract(): lax.dot_general(own_part, other_part, (((0,), (0,)), ((), ())), preferred...  10.9 us
    mul x3, local copies, waits for them, and re-layouts, per_device(): lon_profile[:, None, :, None] * lat_profile[None, :, None, :]  6.26 us
    ppermute x2, starting transfers between devices, from_behind(): return lax.ppermute(block, axis, route)  6.18 us
    unnamed x29, local copies, waits for them, and re-layouts  5.66 us
    dot_general x3, matrix products, per_device(): lax.dot_general(flatten(near_vectors), tapered, (((1,), (1,)), ((), ())),...  5.28 us
    ppermute x2, starting transfers between devices, from_behind_2(): lax.ppermute(value, axis, [(i, (i + by) % devices) for i in range(devices)])  4.7 us
    reduce_sum x3, other arithmetic, anomalies(): jnp.mean(members, axis=0, keepdims=True)  3.38 us
    ppermute x2, waiting for transfers between devices, from_behind_2(): lax.ppermute(value, axis, [(i, (i + by) % devices) for i in range(devices)])  3.32 us
  transfers between devices with their start and end apart: 4, of which 2 were waited for; matrix products, arithmetic and copies ran while one was open for 27% of the time, Pallas kernels for 0%

commit v1 on v0

v1 whole, which is shorter than its diff:
```python
import functools

import jax
import jax.numpy as jnp
from jax import lax
from jax.experimental import pallas as pl
from jax.experimental.pallas import tpu as pltpu
from jax.sharding import PartitionSpec as P

MESH = pl.DeviceIdType.MESH
F32, BF16 = jnp.float32, jnp.bfloat16


def profile(distance, extent):
    ratio = distance.astype(F32) / extent
    return jnp.where(jnp.abs(distance) <= extent, 1.0 - 0.75 * ratio * ratio, 0.0)


def iota(shape, dim):
    return lax.broadcasted_iota(jnp.int32, shape, dim)


def kernel(
    sizes, w_ref, fine_ref, coarse_ref, inc_ref, out_ref,
    fine_in, coarse_in, inc_in, wide, own, west, east, rim_out, rim_in,
    near, near_inc, own_t, near_rim, rim_inc, taper, rim_taper, refine_rim, acc,
    in_sem, send_sem, recv_sem, rim_send_sem, rim_recv_sem,
):
    n_lon, n_lat, kf, kc, nv, lons, lats = sizes
    halves, reach, lon_reach = lons // 2, lats // 8, lons - 1
    members = 2 * kf + kc
    col = kf + nv
    groups = kc // kf
    body = lon_reach * col + halves * kc
    coarse_at = lon_reach * col
    lon, lat = lax.axis_index("lon"), lax.axis_index("lat")
    sides = (lax.rem(lon + n_lon - 1, n_lon), lon, lax.rem(lon + 1, n_lon))
    has = (lat > 0, lat < n_lat - 1)

    barrier = pltpu.get_barrier_semaphore()

    def greet(to_lon, to_lat):
        pl.semaphore_signal(barrier, inc=1, device_id=(to_lon, to_lat), device_id_type=MESH)

    greet(sides[0], lat)
    greet(sides[2], lat)
    for s in range(2):
        @pl.when(has[s])
        def _():
            for t in range(3):
                greet(sides[t], lat + 2 * s - 1)

    loads = [
        pltpu.make_async_copy(src, dst, in_sem.at[n])
        for n, (src, dst) in enumerate(
            ((fine_ref, fine_in), (coarse_ref, coarse_in), (inc_ref, inc_in))
        )
    ]
    for load in loads:
        load.start()

    f_at, c_at, i_at = 0, kf * lons, kf * lons + kc * halves

    def column_at(a):
        return a * col if a < lon_reach else body

    loads[0].wait()
    wide[f_at:f_at + kf * lons] = fine_in[...].astype(F32)
    loads[1].wait()
    wide[c_at:c_at + kc * halves] = coarse_in[...].astype(F32)
    loads[2].wait()
    wide[i_at:i_at + nv * lons] = inc_in[...].astype(F32)

    fine_own, inc_own, coarse_own = [], [], []
    for a in range(lons):
        values = wide[pl.ds(f_at + a, kf, stride=lons), :]
        anom = (values - jnp.mean(values, axis=0, keepdims=True)).astype(BF16)
        vectors = wide[pl.ds(i_at + a, nv, stride=lons), :].astype(BF16)
        at = column_at(a)
        own[at:at + kf] = anom
        own[at + kf:at + col] = vectors
        fine_own.append(anom)
        inc_own.append(vectors)
    for c in range(halves):
        values = wide[pl.ds(c_at + c, kc, stride=halves), :]
        own[coarse_at + c * kc:coarse_at + (c + 1) * kc] = values.astype(BF16)
        coarse_own.append(values)

    lane = iota((kf, lats), 1)
    packs = (
        [v.astype(F32) for v in fine_own] + [v.astype(F32) for v in inc_own],
        [coarse_own[c][g * kf:(g + 1) * kf] for g in range(groups) for c in range(halves)],
    )
    for part in range(2):
        low = high = jnp.zeros((kf, lats), F32)
        for q, values in enumerate(packs[part]):
            here = (lane // reach) == q
            low = jnp.where(here, pltpu.roll(values, (reach * q) % lats, 1), low)
            high = jnp.where(here, pltpu.roll(values, (reach * (q + 1)) % lats, 1), high)
        rim_out[0, part * kf:(part + 1) * kf] = low.astype(BF16)
        rim_out[1, part * kf:(part + 1) * kf] = high.astype(BF16)

    for s in range(2):
        @pl.when(jnp.logical_not(has[s]))
        def _():
            rim_in[s] = jnp.zeros(rim_in.shape[1:], BF16)

    one = jnp.int32(1)
    pl.semaphore_wait(
        barrier, 2 + 3 * jnp.where(has[0], one, 0) + 3 * jnp.where(has[1], one, 0)
    )

    to_west = pltpu.make_async_remote_copy(
        src_ref=own.at[pl.ds(0, body)], dst_ref=east,
        send_sem=send_sem.at[0], recv_sem=recv_sem.at[1],
        device_id=(sides[0], lat), device_id_type=MESH,
    )
    to_east = pltpu.make_async_remote_copy(
        src_ref=own.at[pl.ds(col, body)], dst_ref=west,
        send_sem=send_sem.at[1], recv_sem=recv_sem.at[0],
        device_id=(sides[2], lat), device_id_type=MESH,
    )
    to_west.start()
    to_east.start()

    def rim_copy(s, t):
        return pltpu.make_async_remote_copy(
            src_ref=rim_out.at[s], dst_ref=rim_in.at[1 - s, 2 - t],
            send_sem=rim_send_sem.at[s, t], recv_sem=rim_recv_sem.at[1 - s, 2 - t],
            device_id=(sides[t], lat + 2 * s - 1), device_id_type=MESH,
        )

    for s in range(2):
        @pl.when(has[s])
        def _():
            for t in range(3):
                rim_copy(s, t).start()

    w_fine = w_ref[0] / (kf - 1)
    w_coarse = w_ref[1] / (kc - 1)
    w_paired = w_ref[1] / (kf - 1)
    lat_profile = profile(iota((lats, lats), 0) - iota((lats, lats), 1), reach)
    for d in range(lon_reach + 1):
        taper[d] = lat_profile * (1.0 - 0.75 * (d / lon_reach) * (d / lon_reach))

    block = lons * reach
    shape = (2 * block, lats)
    row, lane = iota(shape, 0), iota(shape, 1)
    side, a_row, i_row = row // block, (row % block) // reach, row % reach
    b_lane, l_lane = lane // reach, lane % reach
    for s in range(2):
        d_lat = i_row - l_lane + reach if s == 0 else reach + l_lane - i_row
        in_lat = jnp.where((side == s) & (b_lane < lons), profile(d_lat, reach), 0.0)
        for t in range(3):
            d_lon = (t - 1) * lons + b_lane - a_row
            n = s * 3 + t
            rim_taper[:, n * lats:(n + 1) * lats] = in_lat * profile(d_lon, lon_reach)

    shape = (2 * lats, lats)
    row, lane = iota(shape, 0), iota(shape, 1)
    place = (row // lats) * halves + (row // reach) % halves
    step = jnp.abs(2 * place - lane // reach)
    weight = jnp.where(step == 0, 1.0, jnp.where(step == 1, 0.5, 0.0))
    weight = jnp.where((row % reach == lane % reach) & (lane < block), weight, 0.0)
    for g in range(groups):
        mine = (row % lats) // (reach * halves) == g
        refine_rim[:, g * lats:(g + 1) * lats] = jnp.where(mine, weight, 0.0).astype(BF16)

    def coarse_parts(refined):
        coarse_anom = refined - jnp.mean(refined, axis=0, keepdims=True)
        pair = refined[:kf]
        return coarse_anom, pair - jnp.mean(pair, axis=0, keepdims=True)

    def set_near(b, fine_anom, refined, vectors):
        coarse_anom, paired = coarse_parts(refined)
        lanes = slice((b + lon_reach) * lats, (b + lon_reach + 1) * lats)
        near[:kf, lanes] = fine_anom
        near[kf:kf + kc, lanes] = coarse_anom.astype(BF16)
        near[kf + kc:, lanes] = paired.astype(BF16)
        near_inc[:, lanes] = vectors
        return coarse_anom, paired

    def set_own(a, refined):
        coarse_anom, paired = set_near(a, fine_own[a], refined, inc_own[a])
        scaled = jnp.concatenate(
            (w_fine * fine_own[a].astype(F32), w_coarse * coarse_anom, -w_paired * paired),
            axis=0,
        )
        own_t[a * lats:(a + 1) * lats] = scaled.T.astype(BF16)

    def add(b, first, last):
        lanes = slice((b + lon_reach) * lats, (b + lon_reach + 1) * lats)
        gram = jnp.dot(
            own_t[first * lats:last * lats], near[:, lanes], preferred_element_type=F32
        )
        tapered = jnp.concatenate(
            [
                (gram[(a - first) * lats:(a - first + 1) * lats] * taper[abs(a - b)]).astype(BF16)
                for a in range(first, last)
            ],
            axis=0,
        )
        acc[:, first * lats:last * lats] += lax.dot_general(
            near_inc[:, lanes], tapered, (((1,), (1,)), ((), ())), preferred_element_type=F32
        )

    acc[...] = jnp.zeros_like(acc)
    for a in range(lon_reach):
        left = coarse_own[a // 2]
        set_own(a, left if a % 2 == 0 else 0.5 * (left + coarse_own[a // 2 + 1]))
    for b in range(lon_reach):
        add(b, 0, lon_reach)

    to_west.wait_recv()
    east_c = [
        east[coarse_at + c * kc:coarse_at + (c + 1) * kc].astype(F32) for c in range(halves)
    ]
    set_own(lon_reach, 0.5 * (coarse_own[halves - 1] + east_c[0]))
    add(lon_reach, 0, lons)
    for b in range(lon_reach):
        add(b, lon_reach, lons)
    for b in range(lon_reach):
        left = east_c[b // 2]
        refined = left if b % 2 == 0 else 0.5 * (left + east_c[b // 2 + 1])
        set_near(
            lons + b, east[b * col:b * col + kf], refined, east[b * col + kf:(b + 1) * col]
        )
        add(lons + b, b + 1, lons)

    to_east.wait_recv()
    west_at = coarse_at - col
    west_c = [
        west[west_at + c * kc:west_at + (c + 1) * kc].astype(F32) for c in range(halves)
    ] + [coarse_own[0]]
    for b in range(1, lons):
        left = west_c[b // 2]
        refined = left if b % 2 == 0 else 0.5 * (left + west_c[b // 2 + 1])
        at = (b - 1) * col if b < lon_reach else body - col
        set_near(b - lons, west[at:at + kf], refined, west[at + kf:at + col])
        add(b - lons, 0, b)

    for s in range(2):
        @pl.when(has[s])
        def _():
            for t in range(3):
                rim_copy(1 - s, 2 - t).wait_recv()

    pairs = []
    for s in range(2):
        for t in range(3):
            pairs.append(
                jnp.concatenate((rim_in[s, t, kf:], rim_in[s, min(t + 1, 2), kf:]), axis=1)
            )
    refined_rim = jnp.dot(
        jnp.concatenate(pairs, axis=0), refine_rim[...], preferred_element_type=F32
    )
    for s in range(2):
        for t in range(3):
            n = s * 3 + t
            lanes = slice(n * lats, (n + 1) * lats)
            refined = jnp.concatenate(
                [
                    refined_rim[n * kf:(n + 1) * kf, g * lats:(g + 1) * lats]
                    for g in range(groups)
                ],
                axis=0,
            )
            coarse_anom, paired = coarse_parts(refined)
            near_rim[:kf, lanes] = rim_in[s, t, :kf]
            near_rim[kf:kf + kc, lanes] = coarse_anom.astype(BF16)
            near_rim[kf + kc:, lanes] = paired.astype(BF16)
            rim_inc[:, lanes] = pltpu.roll(
                rim_in[s, t, :kf].astype(F32), lats - block, 1
            ).astype(BF16)
    own_rim = jnp.concatenate(
        [
            own_t[a * lats + s * (lats - reach):a * lats + s * (lats - reach) + reach]
            for s in range(2)
            for a in range(lons)
        ],
        axis=0,
    )
    gram = jnp.dot(own_rim, near_rim[...], preferred_element_type=F32)
    tapered = (gram * rim_taper[...]).astype(BF16)
    edge = lax.dot_general(
        rim_inc[...], tapered, (((1,), (1,)), ((), ())), preferred_element_type=F32
    )
    lane = iota((nv, lats), 1)
    for a in range(lons):
        low = pltpu.roll(edge, (lats - reach * a) % lats, 1)
        high = pltpu.roll(edge, (2 * lats - reach - block - reach * a) % lats, 1)
        total = acc[:, a * lats:(a + 1) * lats]
        total += jnp.where(lane < reach, low, 0.0) + jnp.where(lane >= lats - reach, high, 0.0)
        out_ref[pl.ds(a, nv, stride=lons), :] = total

    to_west.wait_send()
    to_east.wait_send()
    for s in range(2):
        @pl.when(has[s])
        def _():
            for t in range(3):
                rim_copy(s, t).wait_send()


def solution(mesh):
    n_lon, n_lat = mesh.shape["lon"], mesh.shape["lat"]

    def per_device(fine, coarse, inc, weights):
        kf, lons, lats = fine.shape
        kc, halves, _ = coarse.shape
        nv = inc.shape[0]
        members, col, near_lons = 2 * kf + kc, kf + nv, 3 * lons - 2
        body = (lons - 1) * col + halves * kc
        assert nv == kf and 2 * lons * (lats // 8) == lats and kc * halves == 2 * lons * kf
        result = pl.pallas_call(
            functools.partial(kernel, (n_lon, n_lat, kf, kc, nv, lons, lats)),
            out_shape=jax.ShapeDtypeStruct((nv * lons, lats), F32),
            in_specs=[pl.BlockSpec(memory_space=pltpu.SMEM)]
            + [pl.BlockSpec(memory_space=pl.ANY)] * 3,
            out_specs=pl.BlockSpec(memory_space=pltpu.VMEM),
            scratch_shapes=[
                pltpu.VMEM((kf * lons, lats), BF16),
                pltpu.VMEM((kc * halves, lats), BF16),
                pltpu.VMEM((nv * lons, lats), BF16),
                pltpu.VMEM((col * lons + kc * halves, lats), F32),
                pltpu.VMEM((body + col, lats), BF16),
                pltpu.VMEM((body, lats), BF16),
                pltpu.VMEM((body, lats), BF16),
                pltpu.VMEM((2, 2 * kf, lats), BF16),
                pltpu.VMEM((2, 3, 2 * kf, lats), BF16),
                pltpu.VMEM((members, near_lons * lats), BF16),
                pltpu.VMEM((nv, near_lons * lats), BF16),
                pltpu.VMEM((lons * lats, members), BF16),
                pltpu.VMEM((members, 6 * lats), BF16),
                pltpu.VMEM((nv, 6 * lats), BF16),
                pltpu.VMEM((lons, lats, lats), F32),
                pltpu.VMEM((lats, 6 * lats), F32),
                pltpu.VMEM((2 * lats, (kc // kf) * lats), BF16),
                pltpu.VMEM((nv, lons * lats), F32),
                pltpu.SemaphoreType.DMA((3,)),
                pltpu.SemaphoreType.DMA((2,)),
                pltpu.SemaphoreType.DMA((2,)),
                pltpu.SemaphoreType.DMA((2, 3)),
                pltpu.SemaphoreType.DMA((2, 3)),
            ],
            compiler_params=pltpu.CompilerParams(collective_id=0, has_side_effects=True),
            name="covariance",
        )(
            weights,
            fine.reshape(kf * lons, lats),
            coarse.reshape(kc * halves, lats),
            inc.reshape(nv * lons, lats),
        )
        return result.reshape(nv, lons, lats)

    spec = P(None, "lon", "lat")
    return jax.shard_map(
        per_device, mesh=mesh, in_specs=(spec, spec, spec, P()), out_specs=spec, check_vma=False
    )
```

time: 70.4 us -> 14.3 us (0.20)
  local copies, waits for them, and re-layouts: 26.9 us -> 1.47 us
  matrix products: 16.1 us -> 0 us
  Pallas kernels: 0 us -> 12.6 us
  starting transfers between devices: 10.9 us -> 0 us
  other arithmetic: 10.2 us -> 0 us
  waiting for transfers between devices: 3.32 us -> 0 us
  between operations: 2.14 us -> 0.01 us
    dot_general x9 -> x0, matrix products: 16.1 us -> none  [the longest x6 10.9 us: contract(): lax.dot_general(own_part, other_part, (((0,), (0,)), ((), ())), preferred...]
    pallas_call x0 -> x1, Pallas kernels: none -> 12.6 us  [per_device(): pl.pallas_call(functools.partial(kernel, (n_lon, n_lat, kf, kc, nv, lons,...]
    ppermute x4 -> x0, starting transfers between devices: 10.9 us -> none  [the longest x2 6.18 us: from_behind(): return lax.ppermute(block, axis, route)]
    slice x16 -> x0, local copies, waits for them, and re-layouts: 7.2 us -> none  [the longest x3 1.95 us: per_device(): member_tile[fine_count:fine_count + coarse_count // 2]]
    reshape x16 -> x0, local copies, waits for them, and re-layouts: 6.4 us -> none  [the longest x6 2.91 us: per_device(): member_tile[fine_count:fine_count + coarse_count // 2]]
    mul x3 -> x0, local copies, waits for them, and re-layouts: 6.26 us -> none  [per_device(): lon_profile[:, None, :, None] * lat_profile[None, :, None, :]]
    unnamed x29 -> x1, local copies, waits for them, and re-layouts: 5.66 us -> 1.47 us
    reduce_sum x3 -> x0, other arithmetic: 3.38 us -> none  [anomalies(): jnp.mean(members, axis=0, keepdims=True)]
  transfers between devices with their start and end apart: 4 -> 0, of which waited for: 2 -> 0; matrix products, arithmetic and copies ran while one was open for 27% -> 0% of each run, Pallas kernels for 0% -> 0%
where the time goes in v1:
time: 14.3 us; the launch traced here: 14.1 us
  Pallas kernels  12.6 us (88%)
  local copies, waits for them, and re-layouts  1.47 us (10%)
    pallas_call x1, Pallas kernels, per_device(): pl.pallas_call(functools.partial(kernel, (n_lon, n_lat, kf, kc, nv, lons,...  12.6 us
    unnamed x1, local copies, waits for them, and re-layouts  1.47 us

profile of v1, /device:TPU:0, one launch (start us, length us, event | category | flops | bytes accessed | tf_op | source)
XLA Modules:
  0.0 14.1 jit_solution(9876391033164672272)
XLA Ops:
  0.0 12.6 %covariance.1 = f32[128,128]{1,0:T(8,128)} custom-call(f32[2]{0:T(128)} %w_ref.1, bf16[128,128]{1,0:T(8,128)(2,1)} %bitcast.6, bf16[256,128]{1,0:T(8,128)(2,1)} %bitcast.5, bf16[128,128]{1,0:T(8,128)(2,1)} %bitcast.7), custom_call_target="tpu_custom_call" | custom-call | tf_op jit(solution)/shard_map/covariance/pallas_call | solution.py:315
  12.6 1.5 %copy.6 = f32[32,4,128]{2,1,0:T(4,128)} copy(f32[32,4,128]{2,1,0:T(4,128)} %bitcast.4) | data formatting | bytes 131072

commit v2 on v1

--- a/solution.py
+++ b/solution.py
@@ -21,18 +21,17 @@
 
 
 def kernel(
-    sizes, w_ref, fine_ref, coarse_ref, inc_ref, out_ref,
-    fine_in, coarse_in, inc_in, wide, own, west, east, rim_out, rim_in,
+    sizes, weights_ref, fine_ref, coarse_ref, inc_ref, out_ref,
+    w_ref, fine_in, coarse_in, inc_in, wide, own, own_c, west, east, west_cin, east_cin, rim_out, rim_in,
     near, near_inc, own_t, near_rim, rim_inc, taper, rim_taper, refine_rim, acc,
     in_sem, send_sem, recv_sem, rim_send_sem, rim_recv_sem,
 ):
     n_lon, n_lat, kf, kc, nv, lons, lats = sizes
     halves, reach, lon_reach = lons // 2, lats // 8, lons - 1
-    members = 2 * kf + kc
     col = kf + nv
     groups = kc // kf
-    body = lon_reach * col + halves * kc
-    coarse_at = lon_reach * col
+    body = lon_reach * col
+    ratio = (kc - 1) / (kf - 1)
     lon, lat = lax.axis_index("lon"), lax.axis_index("lat")
     sides = (lax.rem(lon + n_lon - 1, n_lon), lon, lax.rem(lon + 1, n_lon))
     has = (lat > 0, lat < n_lat - 1)
@@ -53,16 +52,13 @@
     loads = [
         pltpu.make_async_copy(src, dst, in_sem.at[n])
         for n, (src, dst) in enumerate(
-            ((fine_ref, fine_in), (coarse_ref, coarse_in), (inc_ref, inc_in))
+            ((fine_ref, fine_in), (coarse_ref, coarse_in), (inc_ref, inc_in), (weights_ref, w_ref))
         )
     ]
     for load in loads:
         load.start()
 
     f_at, c_at, i_at = 0, kf * lons, kf * lons + kc * halves
-
-    def column_at(a):
-        return a * col if a < lon_reach else body
 
     loads[0].wait()
     wide[f_at:f_at + kf * lons] = fine_in[...].astype(F32)
@@ -76,14 +72,14 @@
         values = wide[pl.ds(f_at + a, kf, stride=lons), :]
         anom = (values - jnp.mean(values, axis=0, keepdims=True)).astype(BF16)
         vectors = wide[pl.ds(i_at + a, nv, stride=lons), :].astype(BF16)
-        at = column_at(a)
+        at = a * col
         own[at:at + kf] = anom
         own[at + kf:at + col] = vectors
         fine_own.append(anom)
         inc_own.append(vectors)
     for c in range(halves):
         values = wide[pl.ds(c_at + c, kc, stride=halves), :]
-        own[coarse_at + c * kc:coarse_at + (c + 1) * kc] = values.astype(BF16)
+        own_c[c * kc:(c + 1) * kc] = values.astype(BF16)
         coarse_own.append(values)
 
     lane = iota((kf, lats), 1)
@@ -110,18 +106,18 @@
         barrier, 2 + 3 * jnp.where(has[0], one, 0) + 3 * jnp.where(has[1], one, 0)
     )
 
-    to_west = pltpu.make_async_remote_copy(
-        src_ref=own.at[pl.ds(0, body)], dst_ref=east,
-        send_sem=send_sem.at[0], recv_sem=recv_sem.at[1],
-        device_id=(sides[0], lat), device_id_type=MESH,
-    )
-    to_east = pltpu.make_async_remote_copy(
-        src_ref=own.at[pl.ds(col, body)], dst_ref=west,
-        send_sem=send_sem.at[1], recv_sem=recv_sem.at[0],
-        device_id=(sides[2], lat), device_id_type=MESH,
-    )
-    to_west.start()
-    to_east.start()
+    def send(src, dst, n, towards):
+        return pltpu.make_async_remote_copy(
+            src_ref=src, dst_ref=dst, send_sem=send_sem.at[n], recv_sem=recv_sem.at[n],
+            device_id=(sides[towards], lat), device_id_type=MESH,
+        )
+
+    coarse_west = send(own_c, east_cin, 0, 0)
+    coarse_east = send(own_c, west_cin, 1, 2)
+    rest_west = send(own.at[pl.ds(0, body)], east, 2, 0)
+    rest_east = send(own.at[pl.ds(col, body)], west, 3, 2)
+    coarse_west.start()
+    coarse_east.start()
 
     def rim_copy(s, t):
         return pltpu.make_async_remote_copy(
@@ -133,13 +129,16 @@
     for s in range(2):
         @pl.when(has[s])
         def _():
-            for t in range(3):
+            for t in (0, 2, 1):
                 rim_copy(s, t).start()
 
-    w_fine = w_ref[0] / (kf - 1)
+    rest_west.start()
+    rest_east.start()
+
+    loads[3].wait()
     w_coarse = w_ref[1] / (kc - 1)
-    w_paired = w_ref[1] / (kf - 1)
-    lat_profile = profile(iota((lats, lats), 0) - iota((lats, lats), 1), reach)
+    fine_ratio = ratio * w_ref[0] / w_ref[1]
+    lat_profile = w_coarse * profile(iota((lats, lats), 0) - iota((lats, lats), 1), reach)
     for d in range(lon_reach + 1):
         taper[d] = lat_profile * (1.0 - 0.75 * (d / lon_reach) * (d / lon_reach))
 
@@ -150,7 +149,7 @@
     b_lane, l_lane = lane // reach, lane % reach
     for s in range(2):
         d_lat = i_row - l_lane + reach if s == 0 else reach + l_lane - i_row
-        in_lat = jnp.where((side == s) & (b_lane < lons), profile(d_lat, reach), 0.0)
+        in_lat = jnp.where((side == s) & (b_lane < lons), w_coarse * profile(d_lat, reach), 0.0)
         for t in range(3):
             d_lon = (t - 1) * lons + b_lane - a_row
             n = s * 3 + t
@@ -169,27 +168,37 @@
     def coarse_parts(refined):
         coarse_anom = refined - jnp.mean(refined, axis=0, keepdims=True)
         pair = refined[:kf]
-        return coarse_anom, pair - jnp.mean(pair, axis=0, keepdims=True)
-
-    def set_near(b, fine_anom, refined, vectors):
+        paired = pair - jnp.mean(pair, axis=0, keepdims=True)
+        return coarse_anom.astype(BF16), paired.astype(BF16)
+
+    def lanes_of(b):
+        return slice((b + lon_reach) * lats, (b + lon_reach + 1) * lats)
+
+    def set_near(to, lanes, refined):
         coarse_anom, paired = coarse_parts(refined)
-        lanes = slice((b + lon_reach) * lats, (b + lon_reach + 1) * lats)
-        near[:kf, lanes] = fine_anom
-        near[kf:kf + kc, lanes] = coarse_anom.astype(BF16)
-        near[kf + kc:, lanes] = paired.astype(BF16)
-        near_inc[:, lanes] = vectors
+        to[2 * kf:2 * kf + kc, lanes] = coarse_anom
+        to[2 * kf + kc:3 * kf + kc, lanes] = paired
+        to[3 * kf + kc:, lanes] = paired
         return coarse_anom, paired
 
+    def set_fine(b, fine_anom, vectors):
+        near[:kf, lanes_of(b)] = fine_anom
+        near[kf:2 * kf, lanes_of(b)] = fine_anom
+        near_inc[:, lanes_of(b)] = vectors
+
+    def split(scale, values):
+        scaled = scale * values.astype(F32)
+        high = scaled.astype(BF16).astype(F32)
+        return [high, scaled - high]
+
     def set_own(a, refined):
-        coarse_anom, paired = set_near(a, fine_own[a], refined, inc_own[a])
-        scaled = jnp.concatenate(
-            (w_fine * fine_own[a].astype(F32), w_coarse * coarse_anom, -w_paired * paired),
-            axis=0,
-        )
-        own_t[a * lats:(a + 1) * lats] = scaled.T.astype(BF16)
+        coarse_anom, paired = set_near(near, lanes_of(a), refined)
+        set_fine(a, fine_own[a], inc_own[a])
+        parts = split(fine_ratio, fine_own[a]) + [coarse_anom.astype(F32)] + split(-ratio, paired)
+        own_t[a * lats:(a + 1) * lats] = jnp.concatenate(parts, axis=0).T.astype(BF16)
 
     def add(b, first, last):
-        lanes = slice((b + lon_reach) * lats, (b + lon_reach + 1) * lats)
+        lanes = lanes_of(b)
         gram = jnp.dot(
             own_t[first * lats:last * lats], near[:, lanes], preferred_element_type=F32
         )
@@ -211,33 +220,41 @@
     for b in range(lon_reach):
         add(b, 0, lon_reach)
 
-    to_west.wait_recv()
-    east_c = [
-        east[coarse_at + c * kc:coarse_at + (c + 1) * kc].astype(F32) for c in range(halves)
-    ]
-    set_own(lon_reach, 0.5 * (coarse_own[halves - 1] + east_c[0]))
-    add(lon_reach, 0, lons)
-    for b in range(lon_reach):
-        add(b, lon_reach, lons)
-    for b in range(lon_reach):
-        left = east_c[b // 2]
-        refined = left if b % 2 == 0 else 0.5 * (left + east_c[b // 2 + 1])
-        set_near(
-            lons + b, east[b * col:b * col + kf], refined, east[b * col + kf:(b + 1) * col]
-        )
-        add(lons + b, b + 1, lons)
-
-    to_east.wait_recv()
-    west_at = coarse_at - col
-    west_c = [
-        west[west_at + c * kc:west_at + (c + 1) * kc].astype(F32) for c in range(halves)
-    ] + [coarse_own[0]]
-    for b in range(1, lons):
-        left = west_c[b // 2]
-        refined = left if b % 2 == 0 else 0.5 * (left + west_c[b // 2 + 1])
-        at = (b - 1) * col if b < lon_reach else body - col
-        set_near(b - lons, west[at:at + kf], refined, west[at + kf:at + col])
-        add(b - lons, 0, b)
+    def from_east():
+        coarse_west.wait_recv()
+        east_c = [east_cin[c * kc:(c + 1) * kc].astype(F32) for c in range(halves)]
+        set_own(lon_reach, 0.5 * (coarse_own[halves - 1] + east_c[0]))
+        add(lon_reach, 0, lons)
+        for b in range(lon_reach):
+            add(b, lon_reach, lons)
+        for b in range(lon_reach):
+            left = east_c[b // 2]
+            refined = left if b % 2 == 0 else 0.5 * (left + east_c[b // 2 + 1])
+            set_near(near, lanes_of(lons + b), refined)
+        rest_west.wait_recv()
+        for b in range(lon_reach):
+            at = b * col
+            set_fine(lons + b, east[at:at + kf], east[at + kf:at + col])
+            add(lons + b, b + 1, lons)
+
+    def from_west():
+        coarse_east.wait_recv()
+        west_c = [west_cin[c * kc:(c + 1) * kc].astype(F32) for c in range(halves)]
+        west_c.append(coarse_own[0])
+        for b in range(1, lons):
+            left = west_c[b // 2]
+            refined = left if b % 2 == 0 else 0.5 * (left + west_c[b // 2 + 1])
+            set_near(near, lanes_of(b - lons), refined)
+        rest_east.wait_recv()
+        for b in range(1, lons):
+            at = (b - 1) * col
+            set_fine(b - lons, west[at:at + kf], west[at + kf:at + col])
+            add(b - lons, 0, b)
+
+    is_last = lon == n_lon - 1
+    pl.when(jnp.logical_not(is_last))(from_east)
+    from_west()
+    pl.when(is_last)(from_east)
 
     for s in range(2):
         @pl.when(has[s])
@@ -265,10 +282,9 @@
                 ],
                 axis=0,
             )
-            coarse_anom, paired = coarse_parts(refined)
+            set_near(near_rim, lanes, refined)
             near_rim[:kf, lanes] = rim_in[s, t, :kf]
-            near_rim[kf:kf + kc, lanes] = coarse_anom.astype(BF16)
-            near_rim[kf + kc:, lanes] = paired.astype(BF16)
+            near_rim[kf:2 * kf, lanes] = rim_in[s, t, :kf]
             rim_inc[:, lanes] = pltpu.roll(
                 rim_in[s, t, :kf].astype(F32), lats - block, 1
             ).astype(BF16)
@@ -293,8 +309,8 @@
         total += jnp.where(lane < reach, low, 0.0) + jnp.where(lane >= lats - reach, high, 0.0)
         out_ref[pl.ds(a, nv, stride=lons), :] = total
 
-    to_west.wait_send()
-    to_east.wait_send()
+    for copy in (coarse_west, coarse_east, rest_west, rest_east):
+        copy.wait_send()
     for s in range(2):
         @pl.when(has[s])
         def _():
@@ -309,23 +325,26 @@
         kf, lons, lats = fine.shape
         kc, halves, _ = coarse.shape
         nv = inc.shape[0]
-        members, col, near_lons = 2 * kf + kc, kf + nv, 3 * lons - 2
-        body = (lons - 1) * col + halves * kc
+        members, col, near_lons = 4 * kf + kc, kf + nv, 3 * lons - 2
+        body = (lons - 1) * col
         assert nv == kf and 2 * lons * (lats // 8) == lats and kc * halves == 2 * lons * kf
         result = pl.pallas_call(
             functools.partial(kernel, (n_lon, n_lat, kf, kc, nv, lons, lats)),
-            out_shape=jax.ShapeDtypeStruct((nv * lons, lats), F32),
-            in_specs=[pl.BlockSpec(memory_space=pltpu.SMEM)]
-            + [pl.BlockSpec(memory_space=pl.ANY)] * 3,
+            out_shape=pltpu.VMEM((nv * lons, lats), F32),
+            in_specs=[pl.BlockSpec(memory_space=pl.ANY)] * 4,
             out_specs=pl.BlockSpec(memory_space=pltpu.VMEM),
             scratch_shapes=[
+                pltpu.SMEM(weights.shape, F32),
                 pltpu.VMEM((kf * lons, lats), BF16),
                 pltpu.VMEM((kc * halves, lats), BF16),
                 pltpu.VMEM((nv * lons, lats), BF16),
                 pltpu.VMEM((col * lons + kc * halves, lats), F32),
                 pltpu.VMEM((body + col, lats), BF16),
+                pltpu.VMEM((kc * halves, lats), BF16),
                 pltpu.VMEM((body, lats), BF16),
                 pltpu.VMEM((body, lats), BF16),
+                pltpu.VMEM((kc * halves, lats), BF16),
+                pltpu.VMEM((kc * halves, lats), BF16),
                 pltpu.VMEM((2, 2 * kf, lats), BF16),
                 pltpu.VMEM((2, 3, 2 * kf, lats), BF16),
                 pltpu.VMEM((members, near_lons * lats), BF16),
@@ -337,9 +356,9 @@
                 pltpu.VMEM((lats, 6 * lats), F32),
                 pltpu.VMEM((2 * lats, (kc // kf) * lats), BF16),
                 pltpu.VMEM((nv, lons * lats), F32),
-                pltpu.SemaphoreType.DMA((3,)),
-                pltpu.SemaphoreType.DMA((2,)),
-                pltpu.SemaphoreType.DMA((2,)),
+                pltpu.SemaphoreType.DMA((4,)),
+                pltpu.SemaphoreType.DMA((4,)),
+                pltpu.SemaphoreType.DMA((4,)),
                 pltpu.SemaphoreType.DMA((2, 3)),
                 pltpu.SemaphoreType.DMA((2, 3)),
             ],

time: 14.3 us -> 12.5 us (0.87)
  Pallas kernels: 12.6 us -> 11.7 us
  local copies, waits for them, and re-layouts: 1.47 us -> 0.63 us
    pallas_call x1, Pallas kernels: 12.6 us -> 11.7 us  [per_device(): pl.pallas_call(functools.partial(kernel, (n_lon, n_lat, kf, kc, nv, lons,...]
    unnamed x1, local copies, waits for them, and re-layouts: 1.47 us -> 0.63 us
where the time goes in v2:
time: 12.5 us; the launch traced here: 12.4 us
  Pallas kernels  11.7 us (94%)
  local copies, waits for them, and re-layouts  0.63 us (5%)
    pallas_call x1, Pallas kernels, per_device(): pl.pallas_call(functools.partial(kernel, (n_lon, n_lat, kf, kc, nv, lons,...  11.7 us
    unnamed x1, local copies, waits for them, and re-layouts  0.63 us

profile of v2, /device:TPU:0, one launch (start us, length us, event | category | flops | bytes accessed | tf_op | source)
XLA Modules:
  0.0 12.4 jit_solution(7536147849924667589)
XLA Ops:
  0.0 11.7 %covariance.1 = f32[128,128]{1,0:T(8,128)S(1)} custom-call(f32[2]{0:T(128)} %weights_ref.1, bf16[128,128]{1,0:T(8,128)(2,1)} %bitcast.6, bf16[256,128]{1,0:T(8,128)(2,1)} %bitcast.5, bf16[128,128]{1,0:T(8,128)(2,1)} %bitcast.7), custom_call_target="tpu_custom_call" | custom-call | tf_op jit(solution)/shard_map/covariance/pallas_call | solution.py:331
  11.7 0.6 %copy.6 = f32[32,4,128]{2,1,0:T(4,128)} copy(f32[32,4,128]{2,1,0:T(4,128)S(1)} %bitcast.4) | data formatting | bytes 131072

commit v3 on v2

--- a/solution.py
+++ b/solution.py
@@ -36,6 +36,15 @@
     sides = (lax.rem(lon + n_lon - 1, n_lon), lon, lax.rem(lon + 1, n_lon))
     has = (lat > 0, lat < n_lat - 1)
 
+    loads = [
+        pltpu.make_async_copy(src, dst, in_sem.at[n])
+        for n, (src, dst) in enumerate(
+            ((coarse_ref, coarse_in), (fine_ref, fine_in), (inc_ref, inc_in), (weights_ref, w_ref))
+        )
+    ]
+    for load in loads:
+        load.start()
+
     barrier = pltpu.get_barrier_semaphore()
 
     def greet(to_lon, to_lat):
@@ -49,38 +58,52 @@
             for t in range(3):
                 greet(sides[t], lat + 2 * s - 1)
 
-    loads = [
-        pltpu.make_async_copy(src, dst, in_sem.at[n])
-        for n, (src, dst) in enumerate(
-            ((fine_ref, fine_in), (coarse_ref, coarse_in), (inc_ref, inc_in), (weights_ref, w_ref))
-        )
-    ]
-    for load in loads:
-        load.start()
-
     f_at, c_at, i_at = 0, kf * lons, kf * lons + kc * halves
-
     loads[0].wait()
-    wide[f_at:f_at + kf * lons] = fine_in[...].astype(F32)
-    loads[1].wait()
     wide[c_at:c_at + kc * halves] = coarse_in[...].astype(F32)
-    loads[2].wait()
-    wide[i_at:i_at + nv * lons] = inc_in[...].astype(F32)
-
-    fine_own, inc_own, coarse_own = [], [], []
-    for a in range(lons):
-        values = wide[pl.ds(f_at + a, kf, stride=lons), :]
-        anom = (values - jnp.mean(values, axis=0, keepdims=True)).astype(BF16)
-        vectors = wide[pl.ds(i_at + a, nv, stride=lons), :].astype(BF16)
-        at = a * col
-        own[at:at + kf] = anom
-        own[at + kf:at + col] = vectors
-        fine_own.append(anom)
-        inc_own.append(vectors)
+    coarse_own = []
     for c in range(halves):
         values = wide[pl.ds(c_at + c, kc, stride=halves), :]
         own_c[c * kc:(c + 1) * kc] = values.astype(BF16)
         coarse_own.append(values)
+
+    for s in range(2):
+        @pl.when(jnp.logical_not(has[s]))
+        def _():
+            rim_in[s] = jnp.zeros(rim_in.shape[1:], BF16)
+
+    one = jnp.int32(1)
+    pl.semaphore_wait(
+        barrier, 2 + 3 * jnp.where(has[0], one, 0) + 3 * jnp.where(has[1], one, 0)
+    )
+
+    def send(src, dst, n, towards):
+        return pltpu.make_async_remote_copy(
+            src_ref=src, dst_ref=dst, send_sem=send_sem.at[n], recv_sem=recv_sem.at[n],
+            device_id=(sides[towards], lat), device_id_type=MESH,
+        )
+
+    coarse_west = send(own_c, east_cin, 0, 0)
+    coarse_east = send(own_c, west_cin, 1, 2)
+    rest_west = send(own.at[pl.ds(0, body)], east, 2, 0)
+    rest_east = send(own.at[pl.ds(col, body)], west, 3, 2)
+    coarse_west.start()
+    coarse_east.start()
+
+    fine_own, inc_own = [], []
+    loads[1].wait()
+    wide[f_at:f_at + kf * lons] = fine_in[...].astype(F32)
+    for a in range(lons):
+        values = wide[pl.ds(f_at + a, kf, stride=lons), :]
+        anom = (values - jnp.mean(values, axis=0, keepdims=True)).astype(BF16)
+        own[a * col:a * col + kf] = anom
+        fine_own.append(anom)
+    loads[2].wait()
+    wide[i_at:i_at + nv * lons] = inc_in[...].astype(F32)
+    for a in range(lons):
+        vectors = wide[pl.ds(i_at + a, nv, stride=lons), :].astype(BF16)
+        own[a * col + kf:(a + 1) * col] = vectors
+        inc_own.append(vectors)
 
     lane = iota((kf, lats), 1)
     packs = (
@@ -96,29 +119,6 @@
         rim_out[0, part * kf:(part + 1) * kf] = low.astype(BF16)
         rim_out[1, part * kf:(part + 1) * kf] = high.astype(BF16)
 
-    for s in range(2):
-        @pl.when(jnp.logical_not(has[s]))
-        def _():
-            rim_in[s] = jnp.zeros(rim_in.shape[1:], BF16)
-
-    one = jnp.int32(1)
-    pl.semaphore_wait(
-        barrier, 2 + 3 * jnp.where(has[0], one, 0) + 3 * jnp.where(has[1], one, 0)
-    )
-
-    def send(src, dst, n, towards):
-        return pltpu.make_async_remote_copy(
-            src_ref=src, dst_ref=dst, send_sem=send_sem.at[n], recv_sem=recv_sem.at[n],
-            device_id=(sides[towards], lat), device_id_type=MESH,
-        )
-
-    coarse_west = send(own_c, east_cin, 0, 0)
-    coarse_east = send(own_c, west_cin, 1, 2)
-    rest_west = send(own.at[pl.ds(0, body)], east, 2, 0)
-    rest_east = send(own.at[pl.ds(col, body)], west, 3, 2)
-    coarse_west.start()
-    coarse_east.start()
-
     def rim_copy(s, t):
         return pltpu.make_async_remote_copy(
             src_ref=rim_out.at[s], dst_ref=rim_in.at[1 - s, 2 - t],
@@ -152,7 +152,7 @@
         in_lat = jnp.where((side == s) & (b_lane < lons), w_coarse * profile(d_lat, reach), 0.0)
         for t in range(3):
             d_lon = (t - 1) * lons + b_lane - a_row
-            n = s * 3 + t
+            n = 2 * t + s
             rim_taper[:, n * lats:(n + 1) * lats] = in_lat * profile(d_lon, lon_reach)
 
     shape = (2 * lats, lats)
@@ -220,61 +220,25 @@
     for b in range(lon_reach):
         add(b, 0, lon_reach)
 
-    def from_east():
-        coarse_west.wait_recv()
-        east_c = [east_cin[c * kc:(c + 1) * kc].astype(F32) for c in range(halves)]
-        set_own(lon_reach, 0.5 * (coarse_own[halves - 1] + east_c[0]))
-        add(lon_reach, 0, lons)
-        for b in range(lon_reach):
-            add(b, lon_reach, lons)
-        for b in range(lon_reach):
-            left = east_c[b // 2]
-            refined = left if b % 2 == 0 else 0.5 * (left + east_c[b // 2 + 1])
-            set_near(near, lanes_of(lons + b), refined)
-        rest_west.wait_recv()
-        for b in range(lon_reach):
-            at = b * col
-            set_fine(lons + b, east[at:at + kf], east[at + kf:at + col])
-            add(lons + b, b + 1, lons)
-
-    def from_west():
-        coarse_east.wait_recv()
-        west_c = [west_cin[c * kc:(c + 1) * kc].astype(F32) for c in range(halves)]
-        west_c.append(coarse_own[0])
-        for b in range(1, lons):
-            left = west_c[b // 2]
-            refined = left if b % 2 == 0 else 0.5 * (left + west_c[b // 2 + 1])
-            set_near(near, lanes_of(b - lons), refined)
-        rest_east.wait_recv()
-        for b in range(1, lons):
-            at = (b - 1) * col
-            set_fine(b - lons, west[at:at + kf], west[at + kf:at + col])
-            add(b - lons, 0, b)
-
-    is_last = lon == n_lon - 1
-    pl.when(jnp.logical_not(is_last))(from_east)
-    from_west()
-    pl.when(is_last)(from_east)
-
-    for s in range(2):
-        @pl.when(has[s])
-        def _():
-            for t in range(3):
-                rim_copy(1 - s, 2 - t).wait_recv()
-
-    pairs = []
-    for s in range(2):
-        for t in range(3):
-            pairs.append(
-                jnp.concatenate((rim_in[s, t, kf:], rim_in[s, min(t + 1, 2), kf:]), axis=1)
-            )
-    refined_rim = jnp.dot(
-        jnp.concatenate(pairs, axis=0), refine_rim[...], preferred_element_type=F32
-    )
-    for s in range(2):
-        for t in range(3):
-            n = s * 3 + t
-            lanes = slice(n * lats, (n + 1) * lats)
+    def rim_pack(s, t):
+        return jnp.concatenate((rim_in[s, t, kf:], rim_in[s, min(t + 1, 2), kf:]), axis=1)
+
+    def wait_rims(some):
+        for s in range(2):
+            @pl.when(has[s])
+            def _():
+                for t in some:
+                    rim_copy(1 - s, 2 - t).wait_recv()
+
+    def set_rims(some):
+        order = [(s, t) for s in range(2) for t in some]
+        refined_rim = jnp.dot(
+            jnp.concatenate([rim_pack(s, t) for s, t in order], axis=0),
+            refine_rim[...],
+            preferred_element_type=F32,
+        )
+        for n, (s, t) in enumerate(order):
+            lanes = slice((2 * t + s) * lats, (2 * t + s + 1) * lats)
             refined = jnp.concatenate(
                 [
                     refined_rim[n * kf:(n + 1) * kf, g * lats:(g + 1) * lats]
@@ -288,6 +252,25 @@
             rim_inc[:, lanes] = pltpu.roll(
                 rim_in[s, t, :kf].astype(F32), lats - block, 1
             ).astype(BF16)
+
+    def rim_product(first, last):
+        lanes = slice(2 * first * lats, 2 * last * lats)
+        gram = jnp.dot(own_rim, near_rim[:, lanes], preferred_element_type=F32)
+        tapered = (gram * rim_taper[:, lanes]).astype(BF16)
+        return lax.dot_general(
+            rim_inc[:, lanes], tapered, (((1,), (1,)), ((), ())), preferred_element_type=F32
+        )
+
+    coarse_west.wait_recv()
+    east_c = [east_cin[c * kc:(c + 1) * kc].astype(F32) for c in range(halves)]
+    set_own(lon_reach, 0.5 * (coarse_own[halves - 1] + east_c[0]))
+    add(lon_reach, 0, lons)
+    for b in range(lon_reach):
+        add(b, lon_reach, lons)
+    for b in range(lon_reach):
+        left = east_c[b // 2]
+        refined = left if b % 2 == 0 else 0.5 * (left + east_c[b // 2 + 1])
+        set_near(near, lanes_of(lons + b), refined)
     own_rim = jnp.concatenate(
         [
             own_t[a * lats + s * (lats - reach):a * lats + s * (lats - reach) + reach]
@@ -296,11 +279,33 @@
         ],
         axis=0,
     )
-    gram = jnp.dot(own_rim, near_rim[...], preferred_element_type=F32)
-    tapered = (gram * rim_taper[...]).astype(BF16)
-    edge = lax.dot_general(
-        rim_inc[...], tapered, (((1,), (1,)), ((), ())), preferred_element_type=F32
-    )
+
+    coarse_east.wait_recv()
+    west_c = [west_cin[c * kc:(c + 1) * kc].astype(F32) for c in range(halves)]
+    west_c.append(coarse_own[0])
+    for b in range(1, lons):
+        left = west_c[b // 2]
+        refined = left if b % 2 == 0 else 0.5 * (left + west_c[b // 2 + 1])
+        set_near(near, lanes_of(b - lons), refined)
+
+    rest_west.wait_recv()
+    wait_rims((1, 2))
+    for b in range(lon_reach):
+        at = b * col
+        set_fine(lons + b, east[at:at + kf], east[at + kf:at + col])
+        add(lons + b, b + 1, lons)
+    set_rims((1, 2))
+    edge = rim_product(1, 3)
+
+    rest_east.wait_recv()
+    wait_rims((0,))
+    for b in range(1, lons):
+        at = (b - 1) * col
+        set_fine(b - lons, west[at:at + kf], west[at + kf:at + col])
+        add(b - lons, 0, b)
+    set_rims((0,))
+    edge += rim_product(0, 1)
+
     lane = iota((nv, lats), 1)
     for a in range(lons):
         low = pltpu.roll(edge, (lats - reach * a) % lats, 1)

time: 12.5 us -> 12.6 us (level)
  no operation moved by 1% of the time
where the time goes in v3:
time: 12.6 us; the launch traced here: 12.4 us
  Pallas kernels  11.8 us (94%)
  local copies, waits for them, and re-layouts  0.63 us (5%)
    pallas_call x1, Pallas kernels, per_device(): pl.pallas_call(functools.partial(kernel, (n_lon, n_lat, kf, kc, nv, lons,...  11.8 us
    unnamed x1, local copies, waits for them, and re-layouts  0.63 us

profile of v3, /device:TPU:0, one launch (start us, length us, event | category | flops | bytes accessed | tf_op | source)
XLA Modules:
  0.0 12.4 jit_solution(6848090264305500958)
XLA Ops:
  0.0 11.8 %covariance.1 = f32[128,128]{1,0:T(8,128)S(1)} custom-call(f32[2]{0:T(128)} %weights_ref.1, bf16[128,128]{1,0:T(8,128)(2,1)} %bitcast.6, bf16[256,128]{1,0:T(8,128)(2,1)} %bitcast.5, bf16[128,128]{1,0:T(8,128)(2,1)} %bitcast.7), custom_call_target="tpu_custom_call" | custom-call | tf_op jit(solution)/shard_map/covariance/pallas_call | solution.py:336
  11.8 0.6 %copy.6 = f32[32,4,128]{2,1,0:T(4,128)} copy(f32[32,4,128]{2,1,0:T(4,128)S(1)} %bitcast.4) | data formatting | bytes 131072

commit v4 on v3

--- a/solution.py
+++ b/solution.py
@@ -87,8 +87,8 @@
     coarse_east = send(own_c, west_cin, 1, 2)
     rest_west = send(own.at[pl.ds(0, body)], east, 2, 0)
     rest_east = send(own.at[pl.ds(col, body)], west, 3, 2)
+    coarse_east.start()
     coarse_west.start()
-    coarse_east.start()
 
     fine_own, inc_own = [], []
     loads[1].wait()
@@ -105,6 +105,8 @@
         own[a * col + kf:(a + 1) * col] = vectors
         inc_own.append(vectors)
 
+    rest_east.start()
+    rest_west.start()
     lane = iota((kf, lats), 1)
     packs = (
         [v.astype(F32) for v in fine_own] + [v.astype(F32) for v in inc_own],
@@ -129,11 +131,9 @@
     for s in range(2):
         @pl.when(has[s])
         def _():
-            for t in (0, 2, 1):
+            for t in (2, 0, 1):
                 rim_copy(s, t).start()
 
-    rest_west.start()
-    rest_east.start()
 
     loads[3].wait()
     w_coarse = w_ref[1] / (kc - 1)

time: 12.6 us -> 12.6 us (level)
  no operation moved by 1% of the time
where the time goes in v4:
time: 12.6 us; the launch traced here: 12.4 us
  Pallas kernels  11.8 us (94%)
  local copies, waits for them, and re-layouts  0.63 us (5%)
    pallas_call x1, Pallas kernels, per_device(): pl.pallas_call(functools.partial(kernel, (n_lon, n_lat, kf, kc, nv, lons,...  11.8 us
    unnamed x1, local copies, waits for them, and re-layouts  0.63 us

profile of v4, /device:TPU:0, one launch (start us, length us, event | category | flops | bytes accessed | tf_op | source)
XLA Modules:
  0.0 12.4 jit_solution(12810936097811451200)
XLA Ops:
  0.0 11.8 %covariance.1 = f32[128,128]{1,0:T(8,128)S(1)} custom-call(f32[2]{0:T(128)} %weights_ref.1, bf16[128,128]{1,0:T(8,128)(2,1)} %bitcast.6, bf16[256,128]{1,0:T(8,128)(2,1)} %bitcast.5, bf16[128,128]{1,0:T(8,128)(2,1)} %bitcast.7), custom_call_target="tpu_custom_call" | custom-call | tf_op jit(solution)/shard_map/covariance/pallas_call | solution.py:336
  11.8 0.6 %copy.6 = f32[32,4,128]{2,1,0:T(4,128)} copy(f32[32,4,128]{2,1,0:T(4,128)S(1)} %bitcast.4) | data formatting | bytes 131072
